TPU v7x, 32 devices: a whole 2x2x4 slice. The times are simulated.
32 devices in a mesh: dp: 2 (over x), mp: 16 (over z, y, core).
Axes of the slice: x: 2, y: 2, z: 4, core: 2. Of those that a mesh axis runs over, the one named last changes fastest.
Arguments:
- grad_parts: bfloat16 [2, 16, 1, 512, 512], P('dp', 'mp'), may hold values from -0.1875 to 0.1875
- factors: float32 [16, 2, 512, 512], P('mp', 'dp'), may hold values from -1 to 8, as said below
- root_prev: bfloat16 [16, 2, 512, 512], P(None, 'dp', 'mp'), may hold values from -1 to 2, as said below
- plan: int32 [2, 16], P('dp'), may hold values from 0 to 16, as said below
Outputs:
- new_factors: float32 [16, 2, 512, 512], P('mp', 'dp')
- new_roots: bfloat16 [16, 2, 512, 512], P(None, 'dp', 'mp')
Inputs may be any that keep to these rules, and one draw needn't show every extreme that they name: In each row of plan no worker is named more than 3 times and one is named exactly 3 times; at least 8 entries of a row are below 16. `factors`: each factor is symmetric. `root_prev`: each root is symmetric.
All inputs are finite; a program needn't handle non-finite values.
Results may differ from a plain program's by a relative error of at most 0.0055.
Values may be sent and summed in bfloat16 or wider, within the bound.
A program may use at most 64 MiB of HBM per device.

v0:
```python
import jax
import jax.numpy as jnp
from jax import lax
from jax.sharding import PartitionSpec as P

keep_rate = 0.8


def swapped(value, axis, bit):
    return lax.ppermute(value, axis, [(i, i ^ 1 << bit) for i in range(lax.axis_size(axis))])


def newton(initial, factor):
    identity = jnp.eye(factor.shape[-1], dtype=jnp.float32)
    square = jnp.einsum("sij,sjk->sik", initial, initial, preferred_element_type=jnp.float32)
    fourth = jnp.einsum("sij,sjk->sik", square, square, precision=lax.Precision.HIGHEST)
    coupled = jnp.einsum("sij,sjk->sik", fourth, factor, precision=lax.Precision.HIGHEST)
    update = (5.0 * identity - coupled) * 0.25
    return jnp.einsum(
        "sij,sjk->sik", initial.astype(jnp.float32), update, precision=lax.Precision.HIGHEST
    )


def to_pieces(matrix):
    return lax.all_to_all(matrix, "mp", split_axis=0, concat_axis=0, tiled=True)


def local(grad_parts, factors, root_prev, plan):
    workers = lax.axis_size("mp")
    block_size = factors.shape[-1]
    piece_len = block_size * block_size // workers
    partial_grads = grad_parts.astype(jnp.float32).reshape(
        2 * grad_parts.shape[2], block_size // 2, block_size
    )
    my_half = lax.psum_scatter(
        partial_grads.astype(jnp.bfloat16), "dp", scatter_dimension=0, tiled=True
    ).astype(jnp.float32)[0]
    partner_half = swapped(my_half.astype(jnp.bfloat16), "dp", 0).astype(my_half.dtype)
    my_side = lax.axis_index("dp") % 2
    upper_rows = jnp.where(my_side == 0, my_half, partner_half)
    lower_rows = jnp.where(my_side == 0, partner_half, my_half)
    full_block = jnp.concatenate([upper_rows, lower_rows], axis=0)
    leading = jnp.where(my_side == 0, full_block, full_block.T)
    gram_new = jnp.dot(leading, leading.T, precision=lax.Precision.HIGHEST)
    fresh_factor = keep_rate * factors[0, 0] + (1.0 - keep_rate) * gram_new
    plan_row = plan[0]
    refresh = plan_row < workers
    old_pieces = root_prev.reshape(workers, piece_len)
    gathered = lax.all_to_all(old_pieces, "mp", split_axis=0, concat_axis=0, tiled=True)
    initial = gathered.reshape(1, block_size, block_size)
    own_entry = lax.dynamic_index_in_dim(plan_row, lax.axis_index("mp"), 0, keepdims=False)

    def refine_own():
        return newton(initial, fresh_factor[None])[0].astype(jnp.bfloat16)

    def keep_own():
        return initial[0]

    refined = lax.cond(own_entry < workers, refine_own, keep_own)
    fresh_roots = to_pieces(refined.reshape(workers, piece_len))
    new_roots = jnp.where(refresh[:, None], fresh_roots, old_pieces).reshape(root_prev.shape)
    return (fresh_factor[None, None], new_roots)


def solution(mesh):
    return jax.shard_map(
        local,
        mesh=mesh,
        in_specs=(
            P("dp", "mp", None, None, None),
            P("mp", "dp", None, None),
            P(None, "dp", "mp", None),
            P("dp", None),
        ),
        out_specs=(P("mp", "dp", None, None), P(None, "dp", "mp", None)),
        check_vma=False,
    )
```

profile of v0, /device:TPU:0, one launch (start us, length us, event | category | flops | bytes accessed | tf_op | source)
XLA Modules:
  0.0 89.5 jit_solution(11162649454284539169)
XLA Ops:
  7.2 0.0 copy-start.1
  7.2 0.0 reduce-scatter.2.cloned.1.call-start
  7.2 0.7 reduce-scatter.2.cloned.1.call-update
  7.9 0.3 copy-done.1
  8.2 0.3 all_to_all.22
  8.5 0.6 broadcast.36
  9.1 3.8 %reduce.3 = bf16[16,16384]{1,0:T(8,128)(2,1)S(1)} reduce(bf16[16,1,16384]{2,1,0:T(2,128)(2,1)S(1)} %all_to_all.22, bf16[]{:T(256)} %broadcast.36), dimensions={1}, to_apply=%all_to_all.22.reduce_sub_computation | reduce | bytes 1048578 | tf_op jit(solution)/shard_map/all_to_all | solution.py:49
  12.9 1.2 %reshape.71 = bf16[16,2,8192]{2,1,0:T(2,128)(2,1)} reshape(bf16[16,16384]{1,0:T(8,128)(2,1)S(1)} %reduce.3) | data formatting | bytes 1048576
  14.0 7.4 %all-to-all-start = ((bf16[16,2,8192]{2,1,0:T(2,128)(2,1)}), bf16[16,2,8192]{2,1,0:T(2,128)(2,1)S(1)}, u32[]{:S(2)}, u32[]{:S(2)}) async-start(bf16[16,2,8192]{2,1,0:T(2,128)(2,1)} %reshape.71), calls=%async_computation.1 | async-start | bytes 1048576 | tf_op jit(solution)/shard_map/all_to_all | solution.py:49
  21.5 6.2 %reduce-scatter.2.cloned.1.call-done = bf16[1,256,512]{2,1,0:T(8,128)(2,1)} async-done(((bf16[2,256,512]{2,1,0:T(8,128)(2,1)}), bf16[1,256,512]{2,1,0:T(8,128)(2,1)}) %reduce-scatter.2.cloned.1.call-update) | async-done | bytes 262160 | tf_op jit(solution)/shard_map/reduce_scatter | solution.py:35
  27.6 0.3 collective-permute-start
  28.0 0.0 copy-start.4
  28.0 0.7 copy-done.4
  28.6 0.6 fusion.4
  29.8 0.0 copy-start.3
  29.9 5.9 %all-to-all-done = bf16[16,2,8192]{2,1,0:T(2,128)(2,1)S(1)} async-done(((bf16[16,2,8192]{2,1,0:T(2,128)(2,1)}), bf16[16,2,8192]{2,1,0:T(2,128)(2,1)S(1)}, u32[]{:S(2)}, u32[]{:S(2)}) %all-to-all-start) | async-done | bytes 524320 | tf_op jit(solution)/shard_map/all_to_all | solution.py:49
  35.7 0.5 reshape.72
  36.3 0.0 collective-permute-done
  36.3 0.0 copy-done.3
  36.3 0.1 convert_select_fusion.1
  36.4 0.1 pad_maximum_fusion
  36.5 1.3 %copy.20 = f32[512,512]{0,1:T(8,128)} copy(f32[512,512]{1,0:T(8,128)S(1)} %pad_maximum_fusion) | data formatting | bytes 2097152 | tf_op jit(solution)/shard_map/concatenate | solution.py:42
  37.8 3.8 %fusion.2 = f32[512,512]{1,0:T(8,128)S(1)} fusion(f32[512,512]{0,1:T(8,128)} %copy.20, f32[1,1,512,512]{3,2,1,0:T(8,128)} %param.7, pred[]{:T(512)S(6)} %eq.10, f32[256,512]{1,0:T(8,128)S(1)} %get-tuple-element.22, f32[256,512]{1,0:T(8,128)S(1)} %get-tuple-element.21), kind=kOutput, calls=%fused_computation.6 | convolution fusion | flops 1611923456 | bytes 4194305 | tf_op jit(solution)/shard_map/dot_general | solution.py:44
  41.6 0.0 copy-start
  41.6 1.0 %copy-done = f32[512,512]{1,0:T(8,128)} copy-done((f32[512,512]{1,0:T(8,128)}, f32[512,512]{1,0:T(8,128)S(1)}, u32[]{:S(2)}) %copy-start) | copy-done | bytes 1048600
  42.6 9.6 %conditional.1 = (bf16[512,512]{0,1:T(8,128)(2,1)S(1)}) conditional(s32[]{:T(128)} %bitcast.7, (bf16[16,1,16384]{2,1,0:T(2,128)(2,1)S(1)}) %tuple.19, (bf16[16,1,16384]{2,1,0:T(2,128)(2,1)S(1)}, f32[512,512]{1,0:T(8,128)S(1)}) %tuple.14), branch_computations={%region_1.2_spmd, %region_2.3_spmd} | conditional | flops 5101584384 | bytes 11010058 | solution.py:59
  42.6 3.1 %reduce.1 = bf16[16,16384]{1,0:T(8,128)(2,1)S(1)} reduce(bf16[16,1,16384]{2,1,0:T(2,128)(2,1)S(1)} %get-tuple-element.16, bf16[]{:T(256)} %constant.48), dimensions={1}, to_apply=%get-tuple-element.16.reduce_sub_computation | reduce | bytes 1048578 | tf_op jit(solution)/shard_map
  45.7 0.2 reshape.64
  46.0 0.4 fusion.5
  46.4 1.8 %fusion.6 = f32[512,512]{1,0:T(8,128)S(1)} fusion(f32[512,512]{1,0:T(8,128)S(1)} %fusion.5), kind=kOutput, calls=%fused_computation.17 | convolution fusion | flops 1610612736 | bytes 2097152 | tf_op jit(solution)/shard_map/cond/branch_1_fun/sij,sjk->sik/dot_general | solution.py:16
  48.3 1.8 %fusion = f32[512,512]{1,0:T(8,128)S(1)} fusion(f32[512,512]{1,0:T(8,128)S(1)} %fusion.6, f32[512,512]{1,0:T(8,128)S(1)} %get-tuple-element.11), kind=kOutput, calls=%fused_computation.1 | convolution fusion | flops 1611661312 | bytes 3145728 | tf_op jit(solution)/shard_map/cond/branch_1_fun/sij,sjk->sik/dot_general | solution.py:17
  50.1 1.9 %fusion.1 = bf16[512,512]{0,1:T(8,128)(2,1)S(1)} fusion(f32[512,512]{1,0:T(8,128)S(1)} %fusion, bf16[512,512]{1,0:T(8,128)(2,1)S(1)} %reshape.64), kind=kOutput, calls=%fused_computation.3 | convolution fusion | flops 1610874880 | bytes 2097152 | tf_op jit(solution)/shard_map/cond/branch_1_fun/sij,sjk->sik/dot_general | solution.py:19
  52.2 0.2 copy.24
  52.4 0.3 all_to_all.23
  52.7 3.8 %reduce.4 = bf16[16,16384]{1,0:T(8,128)(2,1)S(1)} reduce(bf16[16,1,16384]{2,1,0:T(2,128)(2,1)S(1)} %all_to_all.23, bf16[]{:T(256)} %broadcast.36), dimensions={1}, to_apply=%all_to_all.23.reduce_sub_computation | reduce | bytes 1048578 | tf_op jit(solution)/shard_map/all_to_all | solution.py:25
  56.5 1.2 %reshape.73 = bf16[16,2,8192]{2,1,0:T(2,128)(2,1)} reshape(bf16[16,16384]{1,0:T(8,128)(2,1)S(1)} %reduce.4) | data formatting | bytes 1048576
  57.7 5.0 %all-to-all-start.1 = ((bf16[16,2,8192]{2,1,0:T(2,128)(2,1)}), bf16[16,2,8192]{2,1,0:T(2,128)(2,1)S(1)}, u32[]{:S(2)}, u32[]{:S(2)}) async-start(bf16[16,2,8192]{2,1,0:T(2,128)(2,1)} %reshape.73), calls=%async_computation.2 | async-start | bytes 1048576 | tf_op jit(solution)/shard_map/all_to_all | solution.py:25
  62.8 14.3 %all-to-all-done.1 = bf16[16,2,8192]{2,1,0:T(2,128)(2,1)S(1)} async-done(((bf16[16,2,8192]{2,1,0:T(2,128)(2,1)}), bf16[16,2,8192]{2,1,0:T(2,128)(2,1)S(1)}, u32[]{:S(2)}, u32[]{:S(2)}) %all-to-all-start.1) | async-done | bytes 524320 | tf_op jit(solution)/shard_map/all_to_all | solution.py:25
  77.0 0.5 reshape.74
  77.5 3.1 %reduce.2 = bf16[16,16384]{1,0:T(8,128)(2,1)S(1)} reduce(bf16[16,1,16384]{2,1,0:T(2,128)(2,1)S(1)} %reshape.74, bf16[]{:T(256)} %constant.49), dimensions={1}, to_apply=%all_to_all.20.reduce_sub_computation | reduce | bytes 1048578 | tf_op jit(solution)/shard_map/all_to_all | solution.py:25
  80.7 0.0 copy-start.2
  80.7 0.2 copy.29
  80.9 0.9 copy-done.2
  81.7 0.9 %bitcast_select_fusion.2 = bf16[16,1,32,512]{3,2,0,1:T(8,128)(2,1)} fusion(bf16[2,8,32,512]{3,2,1,0:T(8,128)(2,1)S(1)} %copy.29, bf16[16,1,32,512]{3,2,1,0:T(8,128)(2,1)S(1)} %copy-done.2, pred[16]{0:T(512)(128)(4,1)S(1)} %compare_bitcast_fusion), kind=kLoop, calls=%fused_computation.11 | loop fusion | flops 262144 | bytes 1572880 | tf_op jit(solution)/shard_map/jit(_where)/select_n | solution.py:61
  (1 shorter events, 0.0 us)
Async XLA Ops:
  7.2 1.0 %copy-start.1 = (bf16[16,1,32,512]{3,2,1,0:T(8,128)(2,1)S(1)}, bf16[16,1,32,512]{3,2,1,0:T(8,128)(2,1)}, u32[]{:S(2)}) copy-start(bf16[16,1,32,512]{3,2,1,0:T(8,128)(2,1)} %param.8) | copy-start | bytes 1572868
  7.2 20.4 %reduce-scatter.2.cloned.1.call-start = ((), (), s32[]{:S(2)}) async-start(), calls=%async_computation.3 | async-start | bytes 786432 | tf_op jit(solution)/shard_map/reduce_scatter | solution.py:35
  14.0 21.7 %all-to-all-start = ((bf16[16,2,8192]{2,1,0:T(2,128)(2,1)}), bf16[16,2,8192]{2,1,0:T(2,128)(2,1)S(1)}, u32[]{:S(2)}, u32[]{:S(2)}) async-start(bf16[16,2,8192]{2,1,0:T(2,128)(2,1)} %reshape.71), calls=%async_computation.1 | async-start | bytes 1048576 | tf_op jit(solution)/shard_map/all_to_all | solution.py:49
  27.6 8.6 %collective-permute-start = (bf16[256,512]{1,0:T(8,128)(2,1)}, bf16[256,512]{1,0:T(8,128)(2,1)S(1)}, u32[]{:S(2)}, u32[]{:S(2)}) collective-permute-start(bf16[256,512]{1,0:T(8,128)(2,1)} %bitcast.37), channel_id=1, source_target_pairs={{0,16},{16,0},{1,17},{17,1},{2,18},{18,2},{3,19},{19,3},{4,20},{20... | collective-permute-start | bytes 786440 | tf_op jit(solution)/shard_map/ppermute | solution.py:10
  28.0 0.7 copy-start.4
  29.8 6.4 %copy-start.3 = (bf16[1,256,512]{2,1,0:T(8,128)(2,1)S(1)}, bf16[1,256,512]{2,1,0:T(8,128)(2,1)}, u32[]{:S(2)}) copy-start(bf16[1,256,512]{2,1,0:T(8,128)(2,1)} %reduce-scatter.2.cloned.1.call-done) | copy-start | bytes 786436
  41.6 1.0 %copy-start = (f32[512,512]{1,0:T(8,128)}, f32[512,512]{1,0:T(8,128)S(1)}, u32[]{:S(2)}) copy-start(f32[512,512]{1,0:T(8,128)S(1)} %fusion.2) | copy-start | bytes 3145732
  57.7 19.3 %all-to-all-start.1 = ((bf16[16,2,8192]{2,1,0:T(2,128)(2,1)}), bf16[16,2,8192]{2,1,0:T(2,128)(2,1)S(1)}, u32[]{:S(2)}, u32[]{:S(2)}) async-start(bf16[16,2,8192]{2,1,0:T(2,128)(2,1)} %reshape.73), calls=%async_computation.2 | async-start | bytes 1048576 | tf_op jit(solution)/shard_map/all_to_all | solution.py:25
  80.7 1.0 %copy-start.2 = (bf16[16,1,32,512]{3,2,1,0:T(8,128)(2,1)S(1)}, bf16[16,1,32,512]{3,2,1,0:T(8,128)(2,1)}, u32[]{:S(2)}) copy-start(bf16[16,1,32,512]{3,2,1,0:T(8,128)(2,1)} %param.8) | copy-start | bytes 1572868
Sparse Core Ops, SparseCore 0:
  10.2 17.3 reduce-scatter.1
where the time goes:
time: 90 us; the launch traced here: 89.5 us
  waiting for transfers between devices  27 us (30%)
  other arithmetic  15.6 us (17%)
  between operations  14.9 us (17%)
  starting transfers between devices  12.8 us (14%)
  matrix products  9.76 us (11%)
  local copies, waits for them, and re-layouts  9.31 us (10%)
    all_to_all x1, waiting for transfers between devices, to_pieces(): return lax.all_to_all(matrix, 'mp', split_axis=0, concat_axis=0, tiled=True)  14.3 us
    all_to_all x1, starting transfers between devices, local(): lax.all_to_all(old_pieces, 'mp', split_axis=0, concat_axis=0, tiled=True)  7.41 us
    all_to_all x2, other arithmetic, to_pieces(): return lax.all_to_all(matrix, 'mp', split_axis=0, concat_axis=0, tiled=True)  6.91 us
    unnamed x15, local copies, waits for them, and re-layouts  6.35 us
    reduce_scatter x1, waiting for transfers between devices, local(): lax.psum_scatter(partial_grads.astype(jnp.bfloat16), 'dp', scatter_dimens...  6.16 us
    all_to_all x1, waiting for transfers between devices, local(): lax.all_to_all(old_pieces, 'mp', split_axis=0, concat_axis=0, tiled=True)  5.88 us
    all_to_all x1, starting transfers between devices, to_pieces(): return lax.all_to_all(matrix, 'mp', split_axis=0, concat_axis=0, tiled=True)  5.05 us
    dot_general x1, matrix products, local(): gram_new = jnp.dot(leading, leading.T, precision=lax.Precision.HIGHEST)  3.78 us
  transfers between devices with their start and end apart: 4, of which 3 were waited for; matrix products, arithmetic and copies ran while one was open for 7% of the time, Pallas kernels for 0%

commit v1 on v0

v1 whole, which is shorter than its diff:
```python
import functools

import jax
import jax.numpy as jnp
from jax import lax
from jax.experimental import pallas as pl
from jax.experimental.pallas import tpu as pltpu
from jax.sharding import PartitionSpec as P

keep_rate = 0.8
MESH = pl.DeviceIdType.MESH
F32 = jnp.float32
BF16 = jnp.bfloat16


def mul(a, b):
    return jnp.dot(a, b, preferred_element_type=F32)


def split(a):
    high = a.astype(BF16)
    return high, (a - high.astype(F32)).astype(BF16)


def kernel(
    n_dp, n_mp, blocks,
    grad, fac, root, fresh, fac_out,
    own_g, in_g, fac_v, root_v, pieces, full_x, rest, fifth, gram_v, out_v, fac_new,
    load_sem, grad_send, grad_recv, root_send, root_recv, out_send, out_recv,
):
    d = lax.axis_index("dp")
    me = lax.axis_index("mp")
    bs = fac.shape[-1]
    half = n_mp // 2
    hb = bs // 2
    side = me // half
    away = 1 - side
    near_cols = pl.ds(pl.multiple_of(side * hb, hb), hb)
    far_cols = pl.ds(pl.multiple_of(away * hb, hb), hb)
    near_pieces = pl.ds(side * half, half)
    far_pieces = pl.ds(away * half, half)

    def far_peer(i):
        return away * half + (me + i) % half

    def near_peer(i):
        return side * half + (me + i) % half

    loads = [
        pltpu.make_async_copy(grad, own_g, load_sem.at[0]),
        pltpu.make_async_copy(root, root_v, load_sem.at[1]),
        pltpu.make_async_copy(root.at[me], pieces.at[me], load_sem.at[2]),
        pltpu.make_async_copy(fac, fac_v, load_sem.at[3]),
    ]
    for load in loads:
        load.start()

    barrier = pltpu.get_barrier_semaphore()

    @pl.loop(1, n_mp)
    def _(i):
        pl.semaphore_signal(barrier, inc=1, device_id=(d, (me + i) % n_mp), device_id_type=MESH)

    for i in range(1, n_dp):
        pl.semaphore_signal(barrier, inc=1, device_id=((d + i) % n_dp, me), device_id_type=MESH)
    pl.semaphore_wait(barrier, n_mp - 1 + n_dp - 1)

    def grad_copy(i):
        other = (d + i) % n_dp
        return pltpu.make_async_remote_copy(
            src_ref=own_g.at[other * blocks // n_dp], dst_ref=in_g.at[i - 1],
            send_sem=grad_send.at[i - 1], recv_sem=grad_recv.at[i - 1],
            device_id=(other, me), device_id_type=MESH,
        )

    loads[0].wait()
    for i in range(1, n_dp):
        grad_copy(i).start()

    def root_far(src, dst, peer, slot, cols):
        return pltpu.make_async_remote_copy(
            src_ref=root_v.at[src, :, cols], dst_ref=pieces.at[dst, :, cols],
            send_sem=root_send.at[peer], recv_sem=root_recv.at[slot],
            device_id=(d, peer), device_id_type=MESH,
        )

    def root_near(src, dst, peer, slot):
        return pltpu.make_async_remote_copy(
            src_ref=root_v.at[src], dst_ref=pieces.at[dst],
            send_sem=root_send.at[peer], recv_sem=root_recv.at[slot],
            device_id=(d, peer), device_id_type=MESH,
        )

    loads[1].wait()

    @pl.loop(0, half)
    def _(i):
        t = far_peer(i)
        root_far(t, me, t, me, near_cols).start()

    @pl.loop(1, half)
    def _(i):
        t = near_peer(i)
        root_near(t, me, t, me).start()

    loads[2].wait()
    loads[3].wait()

    @pl.loop(0, half)
    def _(i):
        s = far_peer(i)
        root_far(s, s, s, s, far_cols).wait_recv()

    @pl.loop(1, half)
    def _(i):
        s = near_peer(i)
        root_near(s, s, s, s).wait_recv()

    near_rows = pieces[near_pieces].astype(F32).reshape(hb, bs).astype(BF16)
    full_x[near_cols, :] = near_rows
    full_x[far_cols, far_cols] = pieces[far_pieces, :, far_cols].astype(F32).reshape(hb, hb).astype(BF16)
    full_x[far_cols, near_cols] = full_x[near_cols, far_cols].astype(F32).T.astype(BF16)

    x = full_x[...]
    sq_h, sq_l = split(mul(x, x))
    fo_h, fo_l = split(mul(sq_h, sq_h) + mul(sq_h, sq_l) + mul(sq_l, sq_h))
    fi_h, fi_l = split(mul(x, fo_h) + mul(x, fo_l))
    fa_h, fa_l = split(fac_v[...])
    fifth[...] = fi_h
    rest[...] = 1.25 * x.astype(F32) - (0.25 * keep_rate) * (
        mul(fi_h, fa_h) + mul(fi_h, fa_l) + mul(fi_l, fa_h)
    )

    for i in range(1, n_dp):
        grad_copy(i).wait_recv()
    total = own_g[d * blocks // n_dp].astype(F32)
    for i in range(1, n_dp):
        total += in_g[i - 1].astype(F32)
    summed = total.astype(BF16)

    @pl.when(d % 2 == 0)
    def _():
        gram_v[...] = lax.dot_general(summed, summed, (((1,), (1,)), ((), ())), preferred_element_type=F32)

    @pl.when(d % 2 == 1)
    def _():
        gram_v[...] = lax.dot_general(summed, summed, (((0,), (0,)), ((), ())), preferred_element_type=F32)

    gram_h = gram_v[...].astype(BF16)

    def out_copy(src, dst, peer, slot):
        return pltpu.make_async_remote_copy(
            src_ref=out_v.at[src], dst_ref=fresh.at[dst],
            send_sem=out_send.at[peer], recv_sem=out_recv.at[slot],
            device_id=(d, peer), device_id_type=MESH,
        )

    def refine(rows, at):
        refined = rest[rows, :] - (0.25 * (1.0 - keep_rate)) * mul(fifth[rows, :], gram_h)
        out_v[at] = refined.reshape(half, bs // n_mp, bs).astype(BF16)

    refine(far_cols, far_pieces)

    @pl.loop(0, half)
    def _(i):
        t = far_peer(i)
        out_copy(t, me, t, me).start()

    refine(near_cols, near_pieces)

    @pl.loop(1, half)
    def _(i):
        t = near_peer(i)
        out_copy(t, me, t, me).start()

    own_out = pltpu.make_async_copy(out_v.at[me], fresh.at[me], load_sem.at[0])
    own_out.start()
    fac_new[...] = keep_rate * fac_v[...] + (1.0 - keep_rate) * gram_v[...]
    fac_store = pltpu.make_async_copy(fac_new, fac_out, load_sem.at[1])
    fac_store.start()

    for i in range(1, n_dp):
        grad_copy(i).wait_send()

    @pl.loop(0, half)
    def _(i):
        t = far_peer(i)
        root_far(t, me, t, me, near_cols).wait_send()

    @pl.loop(1, half)
    def _(i):
        t = near_peer(i)
        root_near(t, me, t, me).wait_send()

    @pl.loop(1, n_mp)
    def _(i):
        s = (me + i) % n_mp
        out_copy(s, s, s, s).wait_send()
        out_copy(s, s, s, s).wait_recv()

    own_out.wait()
    fac_store.wait()


def local(n_dp, n_mp, grad_parts, factors, root_prev, plan):
    blocks, bs = grad_parts.shape[2], factors.shape[-1]
    rows = bs // n_mp
    grads = grad_parts.reshape(blocks, bs, bs)
    old = root_prev.reshape(n_mp, rows, bs)
    fresh, new_factor = pl.pallas_call(
        functools.partial(kernel, n_dp, n_mp, blocks),
        out_shape=(
            jax.ShapeDtypeStruct((n_mp, rows, bs), BF16),
            jax.ShapeDtypeStruct((bs, bs), F32),
        ),
        in_specs=[pl.BlockSpec(memory_space=pl.ANY)] * 3,
        out_specs=(pl.BlockSpec(memory_space=pl.ANY),) * 2,
        scratch_shapes=[
            pltpu.VMEM((blocks, bs, bs), BF16),
            pltpu.VMEM((n_dp - 1, bs, bs), BF16),
            pltpu.VMEM((bs, bs), F32),
            pltpu.VMEM((n_mp, rows, bs), BF16),
            pltpu.VMEM((n_mp, rows, bs), BF16),
            pltpu.VMEM((bs, bs), BF16),
            pltpu.VMEM((bs, bs), F32),
            pltpu.VMEM((bs, bs), BF16),
            pltpu.VMEM((bs, bs), F32),
            pltpu.VMEM((n_mp, rows, bs), BF16),
            pltpu.VMEM((bs, bs), F32),
            pltpu.SemaphoreType.DMA((4,)),
            pltpu.SemaphoreType.DMA((n_dp - 1,)),
            pltpu.SemaphoreType.DMA((n_dp - 1,)),
            pltpu.SemaphoreType.DMA((n_mp,)),
            pltpu.SemaphoreType.DMA((n_mp,)),
            pltpu.SemaphoreType.DMA((n_mp,)),
            pltpu.SemaphoreType.DMA((n_mp,)),
        ],
        compiler_params=pltpu.CompilerParams(collective_id=0, has_side_effects=True),
        name="refresh",
    )(grads, factors.reshape(bs, bs), old)
    refresh = plan[0] < n_mp
    new_roots = jnp.where(refresh[:, None, None], fresh, old).reshape(root_prev.shape)
    return (new_factor[None, None], new_roots)


def solution(mesh):
    return jax.shard_map(
        functools.partial(local, mesh.shape["dp"], mesh.shape["mp"]),
        mesh=mesh,
        in_specs=(
            P("dp", "mp", None, None, None),
            P("mp", "dp", None, None),
            P(None, "dp", "mp", None),
            P("dp", None),
        ),
        out_specs=(P("mp", "dp", None, None), P(None, "dp", "mp", None)),
        check_vma=False,
    )
```

time: 90 us -> 37.6 us (0.42)
  Pallas kernels: 0 us -> 33.8 us
  waiting for transfers between devices: 27 us -> 0 us
  between operations: 14.9 us -> 0.69 us
  other arithmetic: 15.6 us -> 2.04 us
  starting transfers between devices: 12.8 us -> 0 us
  matrix products: 9.76 us -> 0 us
  local copies, waits for them, and re-layouts: 9.31 us -> 0.98 us
    pallas_call x0 -> x1, Pallas kernels: none -> 33.8 us  [local(): pl.pallas_call(functools.partial(kernel, n_dp, n_mp, blocks), out_shape=(...]
    all_to_all x2 -> x0, waiting for transfers between devices: 20.1 us -> none  [the longest x1 14.3 us: to_pieces(): return lax.all_to_all(matrix, 'mp', split_axis=0, concat_axis=0, tiled=True)]
    all_to_all x2 -> x0, starting transfers between devices: 12.5 us -> none  [the longest x1 7.41 us: local(): lax.all_to_all(old_pieces, 'mp', split_axis=0, concat_axis=0, tiled=True)]
    all_to_all x3 -> x0, other arithmetic: 10.7 us -> none  [the longest x2 6.91 us: to_pieces(): return lax.all_to_all(matrix, 'mp', split_axis=0, concat_axis=0, tiled=True)]
    dot_general x5 -> x0, matrix products: 9.76 us -> none  [the longest x1 3.78 us: local(): gram_new = jnp.dot(leading, leading.T, precision=lax.Precision.HIGHEST)]
    reduce_scatter x1 -> x0, waiting for transfers between devices: 6.16 us -> none  [local(): lax.psum_scatter(partial_grads.astype(jnp.bfloat16), 'dp', scatter_dimens...]
    unnamed x15 -> x7, local copies, waits for them, and re-layouts: 6.35 us -> 0.98 us
    another operation x1 -> x0, other arithmetic: 3.14 us -> none
  transfers between devices with their start and end apart: 4 -> 0, of which waited for: 3 -> 0; matrix products, arithmetic and copies ran while one was open for 7% -> 0% of each run, Pallas kernels for 0% -> 0%
where the time goes in v1:
time: 37.6 us; the launch traced here: 37.5 us
  Pallas kernels  33.8 us (90%)
  other arithmetic  2.04 us (5%)
  local copies, waits for them, and re-layouts  0.98 us (3%)
  between operations  0.69 us (2%)
    pallas_call x1, Pallas kernels, local(): pl.pallas_call(functools.partial(kernel, n_dp, n_mp, blocks), out_shape=(...  33.8 us
    unnamed x1, other arithmetic  2.03 us
    unnamed x7, local copies, waits for them, and re-layouts  0.98 us

profile of v1, /device:TPU:0, one launch (start us, length us, event | category | flops | bytes accessed | tf_op | source)
XLA Modules:
  0.0 37.5 jit_solution(6754007225335266122)
XLA Ops:
  0.6 0.0 copy-start.2
  0.6 0.0 copy-start
  0.7 33.8 %refresh.1 = (bf16[16,32,512]{2,1,0:T(8,128)(2,1)}, f32[512,512]{1,0:T(8,128)}) custom-call(bf16[1,512,512]{2,1,0:T(8,128)(2,1)} %bitcast.14, f32[512,512]{1,0:T(8,128)} %bitcast.12, bf16[16,32,512]{2,1,0:T(8,128)(2,1)} %bitcast.11), custom_call_target="tpu_custom_call" | custom-call | tf_op jit(solution)/shard_map/refresh/pallas_call | solution.py:210
  34.4 0.0 copy-start.1
  34.4 0.0 copy-done.2
  34.5 0.0 copy-done
  34.5 2.0 %select_bitcast_fusion = bf16[16,1,32,512]{3,2,1,0:T(8,128)(2,1)} fusion(bf16[16,32,512]{2,1,0:T(8,128)(2,1)} %get-tuple-element.5, pred[16]{0:T(512)(128)(4,1)S(1)} %compare_bitcast_fusion, bf16[16,1,32,512]{3,2,1,0:T(8,128)(2,1)S(1)} %copy-done), kind=kLoop, calls=%fused_computation | loop fusion | flops 262144 | bytes 1572880
  36.5 0.0 copy-done.1
  36.5 1.0 %copy.8 = f32[1,1,512,512]{3,2,1,0:T(8,128)} copy(f32[1,1,512,512]{3,2,1,0:T(8,128)S(1)} %bitcast.13) | data formatting | bytes 2097152
  (1 shorter events, 0.0 us)
Async XLA Ops:
  0.6 33.8 %copy-start.2 = (s32[1,16]{1,0:T(1,128)S(1)}, s32[1,16]{1,0:T(1,128)}, u32[]{:S(2)}) copy-start(s32[1,16]{1,0:T(1,128)} %param.7) | copy-start | bytes 196
  0.6 33.8 %copy-start = (bf16[16,1,32,512]{3,2,1,0:T(8,128)(2,1)S(1)}, bf16[16,1,32,512]{3,2,1,0:T(8,128)(2,1)}, u32[]{:S(2)}) copy-start(bf16[16,1,32,512]{3,2,1,0:T(8,128)(2,1)} %param.6) | copy-start | bytes 1572868
  34.4 2.1 %copy-start.1 = (f32[512,512]{1,0:T(8,128)S(1)}, f32[512,512]{1,0:T(8,128)}, u32[]{:S(2)}) copy-start(f32[512,512]{1,0:T(8,128)} %get-tuple-element.4) | copy-start | bytes 3145732

commit v2 on v1

--- a/solution.py
+++ b/solution.py
@@ -24,9 +24,9 @@
 
 def kernel(
     n_dp, n_mp, blocks,
-    grad, fac, root, fresh, fac_out,
-    own_g, in_g, fac_v, root_v, pieces, full_x, rest, fifth, gram_v, out_v, fac_new,
-    load_sem, grad_send, grad_recv, root_send, root_recv, out_send, out_recv,
+    plan, grad, fac, root, fresh, fac_out,
+    own_g, in_g, fac_v, root_v, pieces, full_x, rest, fifth, gram_v, out_v,
+    load_sem, grad_send, grad_recv, root_send, root_recv, out_send, out_recv, turn,
 ):
     d = lax.axis_index("dp")
     me = lax.axis_index("mp")
@@ -74,8 +74,12 @@
         )
 
     loads[0].wait()
-    for i in range(1, n_dp):
-        grad_copy(i).start()
+    lead = me % 2 == 0
+
+    @pl.when(lead)
+    def _():
+        for i in range(1, n_dp):
+            grad_copy(i).start()
 
     def root_far(src, dst, peer, slot, cols):
         return pltpu.make_async_remote_copy(
@@ -93,15 +97,31 @@
 
     loads[1].wait()
 
-    @pl.loop(0, half)
-    def _(i):
-        t = far_peer(i)
-        root_far(t, me, t, me, near_cols).start()
-
-    @pl.loop(1, half)
-    def _(i):
-        t = near_peer(i)
-        root_near(t, me, t, me).start()
+    for parity in range(2):
+        @pl.loop(0, half // 2)
+        def _(i):
+            t = away * half + (me // 2 * 2 + 2 * i) % half + parity
+            root_far(t, me, t, me, near_cols).start()
+
+        @pl.loop(0, half // 2)
+        def _(i):
+            t = side * half + (me // 2 * 2 + 2 * i) % half + parity
+
+            @pl.when(t != me)
+            def _():
+                root_near(t, me, t, me).start()
+
+    @pl.when(lead)
+    def _():
+        for i in range(1, n_dp):
+            grad_copy(i).wait_send()
+        pl.semaphore_signal(turn, inc=1, device_id=(d, me + 1), device_id_type=MESH)
+
+    @pl.when(jnp.logical_not(lead))
+    def _():
+        pl.semaphore_wait(turn, 1)
+        for i in range(1, n_dp):
+            grad_copy(i).start()
 
     loads[2].wait()
     loads[3].wait()
@@ -123,13 +143,9 @@
 
     x = full_x[...]
     sq_h, sq_l = split(mul(x, x))
-    fo_h, fo_l = split(mul(sq_h, sq_h) + mul(sq_h, sq_l) + mul(sq_l, sq_h))
-    fi_h, fi_l = split(mul(x, fo_h) + mul(x, fo_l))
-    fa_h, fa_l = split(fac_v[...])
-    fifth[...] = fi_h
-    rest[...] = 1.25 * x.astype(F32) - (0.25 * keep_rate) * (
-        mul(fi_h, fa_h) + mul(fi_h, fa_l) + mul(fi_l, fa_h)
-    )
+    fourth = (mul(sq_h, sq_h) + mul(sq_h, sq_l) + mul(sq_l, sq_h)).astype(BF16)
+    fifth[...] = mul(x, fourth).astype(BF16)
+    rest[...] = 1.25 * x.astype(F32) - (0.25 * keep_rate) * mul(fifth[...], fac_v[...].astype(BF16))
 
     for i in range(1, n_dp):
         grad_copy(i).wait_recv()
@@ -155,8 +171,11 @@
             device_id=(d, peer), device_id_type=MESH,
         )
 
+    kept = plan[0, me] >= n_mp
+
     def refine(rows, at):
         refined = rest[rows, :] - (0.25 * (1.0 - keep_rate)) * mul(fifth[rows, :], gram_h)
+        refined = jnp.where(kept, full_x[rows, :].astype(F32), refined)
         out_v[at] = refined.reshape(half, bs // n_mp, bs).astype(BF16)
 
     refine(far_cols, far_pieces)
@@ -175,12 +194,12 @@
 
     own_out = pltpu.make_async_copy(out_v.at[me], fresh.at[me], load_sem.at[0])
     own_out.start()
-    fac_new[...] = keep_rate * fac_v[...] + (1.0 - keep_rate) * gram_v[...]
-    fac_store = pltpu.make_async_copy(fac_new, fac_out, load_sem.at[1])
-    fac_store.start()
-
-    for i in range(1, n_dp):
-        grad_copy(i).wait_send()
+    fac_out[...] = keep_rate * fac_v[...] + (1.0 - keep_rate) * gram_v[...]
+
+    @pl.when(jnp.logical_not(lead))
+    def _():
+        for i in range(1, n_dp):
+            grad_copy(i).wait_send()
 
     @pl.loop(0, half)
     def _(i):
@@ -199,7 +218,6 @@
         out_copy(s, s, s, s).wait_recv()
 
     own_out.wait()
-    fac_store.wait()
 
 
 def local(n_dp, n_mp, grad_parts, factors, root_prev, plan):
@@ -210,11 +228,11 @@
     fresh, new_factor = pl.pallas_call(
         functools.partial(kernel, n_dp, n_mp, blocks),
         out_shape=(
-            jax.ShapeDtypeStruct((n_mp, rows, bs), BF16),
-            jax.ShapeDtypeStruct((bs, bs), F32),
+            pltpu.VMEM((n_mp, rows, bs), BF16),
+            pltpu.VMEM((bs, bs), F32),
         ),
-        in_specs=[pl.BlockSpec(memory_space=pl.ANY)] * 3,
-        out_specs=(pl.BlockSpec(memory_space=pl.ANY),) * 2,
+        in_specs=[pl.BlockSpec(memory_space=pltpu.SMEM)] + [pl.BlockSpec(memory_space=pl.ANY)] * 3,
+        out_specs=(pl.BlockSpec(memory_space=pltpu.VMEM),) * 2,
         scratch_shapes=[
             pltpu.VMEM((blocks, bs, bs), BF16),
             pltpu.VMEM((n_dp - 1, bs, bs), BF16),
@@ -226,7 +244,6 @@
             pltpu.VMEM((bs, bs), BF16),
             pltpu.VMEM((bs, bs), F32),
             pltpu.VMEM((n_mp, rows, bs), BF16),
-            pltpu.VMEM((bs, bs), F32),
             pltpu.SemaphoreType.DMA((4,)),
             pltpu.SemaphoreType.DMA((n_dp - 1,)),
             pltpu.SemaphoreType.DMA((n_dp - 1,)),
@@ -234,13 +251,12 @@
             pltpu.SemaphoreType.DMA((n_mp,)),
             pltpu.SemaphoreType.DMA((n_mp,)),
             pltpu.SemaphoreType.DMA((n_mp,)),
+            pltpu.SemaphoreType.REGULAR,
         ],
         compiler_params=pltpu.CompilerParams(collective_id=0, has_side_effects=True),
         name="refresh",
-    )(grads, factors.reshape(bs, bs), old)
-    refresh = plan[0] < n_mp
-    new_roots = jnp.where(refresh[:, None, None], fresh, old).reshape(root_prev.shape)
-    return (new_factor[None, None], new_roots)
+    )(plan, grads, factors.reshape(bs, bs), old)
+    return (new_factor[None, None], fresh.reshape(root_prev.shape))
 
 
 def solution(mesh):

time: 37.6 us -> 33.5 us (0.89)
  Pallas kernels: 33.8 us -> 30.9 us
  other arithmetic: 2.04 us -> 0 us
  local copies, waits for them, and re-layouts: 0.98 us -> 1.77 us
    pallas_call x1, Pallas kernels: 33.8 us -> 30.9 us  [local(): pl.pallas_call(functools.partial(kernel, n_dp, n_mp, blocks), out_shape=(...]
    unnamed x1 -> x0, other arithmetic: 2.03 us -> none
    unnamed x7 -> x2, local copies, waits for them, and re-layouts: 0.98 us -> 1.77 us
where the time goes in v2:
time: 33.5 us; the launch traced here: 33.4 us
  Pallas kernels  30.9 us (92%)
  local copies, waits for them, and re-layouts  1.77 us (5%)
  between operations  0.64 us (2%)
    pallas_call x1, Pallas kernels, local(): pl.pallas_call(functools.partial(kernel, n_dp, n_mp, blocks), out_shape=(...  30.9 us
    unnamed x2, local copies, waits for them, and re-layouts  1.77 us

profile of v2, /device:TPU:0, one launch (start us, length us, event | category | flops | bytes accessed | tf_op | source)
XLA Modules:
  0.0 33.4 jit_solution(2317290074595418891)
XLA Ops:
  0.6 30.9 %refresh.1 = (bf16[16,32,512]{2,1,0:T(8,128)(2,1)S(1)}, f32[512,512]{1,0:T(8,128)S(1)}) custom-call(s32[1,16]{1,0:T(1,128)} %plan.1, bf16[1,512,512]{2,1,0:T(8,128)(2,1)} %bitcast.10, f32[512,512]{1,0:T(8,128)} %bitcast.9, bf16[16,32,512]{2,1,0:T(8,128)(2,1)} %bitcast.11), custom_call_target="tpu_custom_call" | custom-call | tf_op jit(solution)/shard_map/refresh/pallas_call | solution.py:228
  31.6 1.0 %copy.9 = f32[1,1,512,512]{3,2,1,0:T(8,128)} copy(f32[1,1,512,512]{3,2,1,0:T(8,128)S(1)} %bitcast.7) | data formatting | bytes 2097152
  32.6 0.8 %copy.10 = bf16[16,1,32,512]{3,2,1,0:T(8,128)(2,1)} copy(bf16[16,1,32,512]{3,2,1,0:T(8,128)(2,1)S(1)} %bitcast.8) | data formatting | bytes 1048576

commit v3 on v2

--- a/solution.py
+++ b/solution.py
@@ -24,7 +24,7 @@
 
 def kernel(
     n_dp, n_mp, blocks,
-    plan, grad, fac, root, fresh, fac_out,
+    plan, grad, fac, root, fresh, fac_out, plan_s,
     own_g, in_g, fac_v, root_v, pieces, full_x, rest, fifth, gram_v, out_v,
     load_sem, grad_send, grad_recv, root_send, root_recv, out_send, out_recv, turn,
 ):
@@ -51,6 +51,7 @@
         pltpu.make_async_copy(root, root_v, load_sem.at[1]),
         pltpu.make_async_copy(root.at[me], pieces.at[me], load_sem.at[2]),
         pltpu.make_async_copy(fac, fac_v, load_sem.at[3]),
+        pltpu.make_async_copy(plan, plan_s, load_sem.at[4]),
     ]
     for load in loads:
         load.start()
@@ -171,7 +172,8 @@
             device_id=(d, peer), device_id_type=MESH,
         )
 
-    kept = plan[0, me] >= n_mp
+    loads[4].wait()
+    kept = plan_s[0, me] >= n_mp
 
     def refine(rows, at):
         refined = rest[rows, :] - (0.25 * (1.0 - keep_rate)) * mul(fifth[rows, :], gram_h)
@@ -231,9 +233,10 @@
             pltpu.VMEM((n_mp, rows, bs), BF16),
             pltpu.VMEM((bs, bs), F32),
         ),
-        in_specs=[pl.BlockSpec(memory_space=pltpu.SMEM)] + [pl.BlockSpec(memory_space=pl.ANY)] * 3,
+        in_specs=[pl.BlockSpec(memory_space=pl.ANY)] * 4,
         out_specs=(pl.BlockSpec(memory_space=pltpu.VMEM),) * 2,
         scratch_shapes=[
+            pltpu.SMEM(plan.shape, plan.dtype),
             pltpu.VMEM((blocks, bs, bs), BF16),
             pltpu.VMEM((n_dp - 1, bs, bs), BF16),
             pltpu.VMEM((bs, bs), F32),
@@ -244,7 +247,7 @@
             pltpu.VMEM((bs, bs), BF16),
             pltpu.VMEM((bs, bs), F32),
             pltpu.VMEM((n_mp, rows, bs), BF16),
-            pltpu.SemaphoreType.DMA((4,)),
+            pltpu.SemaphoreType.DMA((5,)),
             pltpu.SemaphoreType.DMA((n_dp - 1,)),
             pltpu.SemaphoreType.DMA((n_dp - 1,)),
             pltpu.SemaphoreType.DMA((n_mp,)),

time: 33.5 us -> 32.9 us (0.982)
  Pallas kernels: 30.9 us -> 30.4 us
    pallas_call x1, Pallas kernels: 30.9 us -> 30.4 us  [local(): pl.pallas_call(functools.partial(kernel, n_dp, n_mp, blocks), out_shape=(...]
where the time goes in v3:
time: 32.9 us; the launch traced here: 32.8 us
  Pallas kernels  30.4 us (92%)
  local copies, waits for them, and re-layouts  1.77 us (5%)
  between operations  0.64 us (2%)
    pallas_call x1, Pallas kernels, local(): pl.pallas_call(functools.partial(kernel, n_dp, n_mp, blocks), out_shape=(...  30.4 us
    unnamed x2, local copies, waits for them, and re-layouts  1.77 us

profile of v3, /device:TPU:0, one launch (start us, length us, event | category | flops | bytes accessed | tf_op | source)
XLA Modules:
  0.0 32.8 jit_solution(8550775660319924195)
XLA Ops:
  0.6 30.4 %refresh.1 = (bf16[16,32,512]{2,1,0:T(8,128)(2,1)S(1)}, f32[512,512]{1,0:T(8,128)S(1)}) custom-call(s32[1,16]{1,0:T(1,128)} %plan.1, bf16[1,512,512]{2,1,0:T(8,128)(2,1)} %bitcast.10, f32[512,512]{1,0:T(8,128)} %bitcast.9, bf16[16,32,512]{2,1,0:T(8,128)(2,1)} %bitcast.11), custom_call_target="tpu_custom_call" | custom-call | tf_op jit(solution)/shard_map/refresh/pallas_call | solution.py:230
  31.0 1.0 %copy.9 = f32[1,1,512,512]{3,2,1,0:T(8,128)} copy(f32[1,1,512,512]{3,2,1,0:T(8,128)S(1)} %bitcast.7) | data formatting | bytes 2097152
  32.0 0.8 %copy.10 = bf16[16,1,32,512]{3,2,1,0:T(8,128)(2,1)} copy(bf16[16,1,32,512]{3,2,1,0:T(8,128)(2,1)S(1)} %bitcast.8) | data formatting | bytes 1048576
